TPU v7x, 32 devices: a whole 2x2x4 slice. The times are simulated.
32 devices in a mesh: dp: 4 (over y, core), vocab: 8 (over z, x).
Axes of the slice: x: 2, y: 2, z: 4, core: 2. Of those that a mesh axis runs over, the one named last changes fastest.
Arguments:
- student_hidden: bfloat16 [512, 2048], P('dp', 'vocab'), may hold values from -210 to 210
- student_blocks: bfloat16 [8, 1024, 4864], P('vocab', 'dp'), may hold values from -0.375 to 0.375
- teacher_logits: bfloat16 [512, 19456], P('dp', 'vocab'), may hold values from -16 to 308
- token_ids: int32 [512], P('dp'), may hold values from 0 to 19455
- loss_mask: int32 [512], P('dp'), may hold values from 0 to 1, as said below
Outputs:
- hidden_grad: bfloat16 [512, 2048], P('dp', 'vocab')
- token_kl: float32 [512], P('dp')
- sampled_logprob: float32 [512], P('dp')
- loss: float32 [], replicated
Inputs may be any that keep to these rules, and one draw needn't show every extreme that they name: `loss_mask`: in each block of 128 tokens the mask is 0 on a leading run of at most 64 tokens and 1 on the rest.
All inputs are finite; a program needn't handle non-finite values.
Results may differ from a plain program's by a relative error of at most 0.0047.
Values may be sent and summed in bfloat16 or wider, within the bound.
No kernel may reach another device: no remote copies, remote signals or barrier semaphores. Data moves between devices by JAX's collectives and lax.ppermute only.
A program may use at most 64 MiB of HBM per device.

v0:
```python
import jax
import jax.numpy as jnp
from jax import lax
from jax.sharding import PartitionSpec as P

D = 2048
VT = 2432


def swapped(shard, axis, stride):
    return lax.ppermute(shard, axis, [(i, i ^ 1 << stride) for i in range(lax.axis_size(axis))])


def combined_all(part, axis, combine):
    gathered = jax.tree.map(lambda a: lax.all_gather(a, axis), part)

    def take(source):
        return jax.tree.map(lambda a: lax.dynamic_index_in_dim(a, source, 0, False), gathered)

    return lax.fori_loop(
        1, lax.axis_size(axis), lambda source, state: combine(state, take(source)), take(0)
    )


def pair_merge(left_pair, right_pair):
    left_max, left_total = left_pair
    right_max, right_total = right_pair
    top_value = jnp.maximum(left_max, right_max)
    merged_total = left_total * jnp.exp(left_max - top_value) + right_total * jnp.exp(
        right_max - top_value
    )
    return (top_value, merged_total)


def row_stats(values):
    row_max = jnp.max(values, axis=1)
    row_total = jnp.sum(jnp.exp(values - row_max[:, None]), axis=1)
    return (row_max, row_total)


def on_device(student_hidden, student_blocks, teacher_logits, token_ids, loss_mask):
    vocab_index = lax.axis_index("vocab")
    pair_side = vocab_index % 2
    mask_float = loss_mask.astype(jnp.float32)
    mask_total = lax.psum(jnp.sum(mask_float), "dp")
    gathered = lax.all_gather(student_hidden, "vocab", axis=1, tiled=True)
    piece = student_blocks[0]
    own_block = lax.dynamic_slice_in_dim(piece, pair_side * VT, VT, 1)
    far_block = lax.dynamic_slice_in_dim(piece, (1 - pair_side) * VT, VT, 1)
    received = swapped(far_block, "vocab", 0)
    stacked = jnp.where(
        pair_side == 0, jnp.stack([own_block, received]), jnp.stack([received, own_block])
    )
    weight = lax.all_gather(stacked, "dp", axis=1, tiled=True).reshape(D, VT)
    logits = jnp.dot(gathered, weight, preferred_element_type=jnp.float32)
    column_start = vocab_index * VT
    teacher_local = teacher_logits.astype(jnp.float32)
    teacher_full = teacher_logits.astype(jnp.float32)
    teacher_max = lax.pmax(jnp.max(teacher_full, axis=1), "vocab")
    teacher_total = lax.psum(jnp.sum(jnp.exp(teacher_full - teacher_max[:, None]), axis=1), "vocab")
    student_max, student_total = row_stats(logits)
    merged = combined_all((student_max, student_total), "vocab", pair_merge)
    stats = (teacher_max, teacher_total, merged[0], merged[1])
    teacher_logp = teacher_local - stats[0][:, None] - jnp.log(stats[1])[:, None]
    student_logp = logits - stats[2][:, None] - jnp.log(stats[3])[:, None]
    teacher_prob = jnp.exp(teacher_logp)
    kl_part = jnp.sum(teacher_prob * (teacher_logp - student_logp), axis=1)
    columns = lax.broadcasted_iota(jnp.int32, logits.shape, 1) + column_start
    sampled_part = jnp.sum(jnp.where(columns == token_ids[:, None], student_logp, 0.0), axis=1)
    token_kl, sampled = lax.psum((kl_part, sampled_part), "vocab")
    loss = lax.psum(jnp.sum(mask_float * token_kl), "dp") / mask_total
    factor = mask_float / mask_total
    dlogits = (factor[:, None] * (jnp.exp(student_logp) - teacher_prob)).astype(jnp.bfloat16)
    term = lax.dot_general(
        dlogits, weight, (((1,), (1,)), ((), ())), preferred_element_type=jnp.float32
    )
    hidden_grad = lax.psum_scatter(term, "vocab", scatter_dimension=1, tiled=True).astype(
        jnp.bfloat16
    )
    return (hidden_grad, token_kl, sampled, loss)


def solution(mesh):
    return jax.shard_map(
        on_device,
        mesh=mesh,
        in_specs=(P("dp", "vocab"), P("vocab", "dp", None), P("dp", "vocab"), P("dp"), P("dp")),
        out_specs=(P("dp", "vocab"), P("dp"), P("dp"), P()),
        check_vma=False,
    )
```

profile of v0, /device:TPU:0, one launch (start us, length us, event | category | flops | bytes accessed | tf_op | source)
XLA Modules:
  0.0 265.2 jit_solution(2844016320098941567)
XLA Ops:
  7.2 0.0 all-gather.6.cloned.1.call-start
  7.2 2.9 %constant_dynamic-slice_fusion.1 = (bf16[1,256,2432]{2,1,0:T(8,128)(2,1)S(1)}, bf16[256,2432]{1,0:T(8,128)(2,1)}) fusion(bf16[1,256,4864]{2,1,0:T(8,128)(2,1)} %param.8, s32[]{:T(128)S(6)} %select_n.41, s32[]{:T(128)S(6)} %select_n.42), kind=kLoop, calls=%fused_computation.33 | loop fusion | bytes 4980744 | tf_op jit(solution)/shard_map/dynamic_slice | solution.py:48
  10.1 3.0 %collective-permute-start = (bf16[256,2432]{1,0:T(8,128)(2,1)}, bf16[256,2432]{1,0:T(8,128)(2,1)S(1)}, u32[]{:S(2)}, u32[]{:S(2)}) collective-permute-start(bf16[256,2432]{1,0:T(8,128)(2,1)} %get-tuple-element.160), channel_id=1, source_target_pairs={{0,1},{1,0},{2,3},{3,2},{4,5},{5,4},{6,7},{7,6},{8,9},{9,8},{10,11... | collective-permute-start | bytes 3735560 | tf_op jit(solution)/shard_map/ppermute | solution.py:11
  13.1 27.6 %collective-permute-done = bf16[256,2432]{1,0:T(8,128)(2,1)S(1)} collective-permute-done((bf16[256,2432]{1,0:T(8,128)(2,1)}, bf16[256,2432]{1,0:T(8,128)(2,1)S(1)}, u32[]{:S(2)}, u32[]{:S(2)}) %collective-permute-start) | collective-permute-done | bytes 1245216 | tf_op jit(solution)/shard_map/ppermute | solution.py:11
  40.7 1.8 maximum_select_fusion
  42.5 0.0 copy-start
  42.5 0.0 all-gather.6.cloned.1.call-update
  42.5 0.0 reduce-scatter.2.cloned.1.call-start
  42.6 1.0 copy-done
  43.6 0.0 copy-start.1
  43.6 0.3 copy.10
  43.9 0.2 reduce_max.24
  44.1 21.9 %pmax.7 = f32[128]{0:T(128)S(1)} all-reduce(bf16[128]{0:T(256)(128)(2,1)S(1)} %reduce_max.24), channel_id=1, replica_groups=mesh['dp'=4,'vocab'=8] {'vocab'}, use_global_device_ids=true, to_apply=%region_7.8 | all-reduce | flops 128 | bytes 768 | tf_op jit(solution)/shard_map/pmax | solution.py:59
  66.0 0.3 exponential_reduce_fusion
  66.3 17.1 %psum.36 = f32[128]{0:T(128)S(1)} all-reduce(f32[128]{0:T(128)S(1)} %exponential_reduce_fusion), channel_id=1, replica_groups=mesh['dp'=4,'vocab'=8] {'vocab'}, use_global_device_ids=true, to_apply=%region_9.10 | all-reduce | flops 128 | bytes 1024 | tf_op jit(solution)/shard_map/psum | solution.py:60
  83.5 0.0 copy-done.1
  83.5 31.2 %all_gather.19 = bf16[128,2048]{1,0:T(8,128)(2,1)S(1)} all-gather(bf16[128,256]{1,0:T(8,128)(2,1)S(1)} %copy-done.1), channel_id=1, replica_groups=mesh['dp'=4,'vocab'=8] {'vocab'}, dimensions={1}, use_global_device_ids=true | all-gather | bytes 589824 | tf_op jit(solution)/shard_map/all_gather | solution.py:46
  114.7 0.0 all-gather.6.cloned.1.call-done
  114.7 6.6 %fusion.17 = (f32[128]{0:T(128)S(1)}, f32[2432,128]{1,0:T(8,128)S(1)}) fusion(bf16[2048,2432]{1,0:T(8,128)(2,1)} %bitcast.46, bf16[128,2048]{1,0:T(8,128)(2,1)S(1)} %all_gather.19), kind=kOutput, calls=%fused_computation.36 | convolution fusion | flops 1275379584 | bytes 11731456 | tf_op jit(solution)/shard_map/dot_general | solution.py:55
  121.4 0.0 copy-start.2
  121.4 0.3 exponential_reduce_fusion.1
  121.7 0.0 copy-start.3
  121.7 18.5 %all-gather.3 = f32[8,1,128]{2,1,0:T(1,128)S(1)} all-gather(f32[1,1,128]{2,1,0:T(1,128)S(1)} %bitcast.52), channel_id=3, replica_groups=mesh['dp'=4,'vocab'=8] {'vocab'}, dimensions={0}, use_global_device_ids=true | all-gather | bytes 4608 | tf_op jit(solution)/shard_map/all_gather | solution.py:15
  140.2 16.3 %all-gather.2 = f32[8,1,128]{2,1,0:T(1,128)S(1)} all-gather(f32[1,1,128]{2,1,0:T(1,128)S(1)} %bitcast.51), channel_id=2, replica_groups=mesh['dp'=4,'vocab'=8] {'vocab'}, dimensions={0}, use_global_device_ids=true | all-gather | bytes 4608 | tf_op jit(solution)/shard_map/all_gather | solution.py:15
  156.5 0.3 while.17
  156.8 0.0 copy-done.2
  156.8 1.1 fusion.7
  157.9 19.7 %all-reduce = (f32[128]{0:T(128)S(1)}, f32[128]{0:T(128)}) all-reduce(f32[128]{0:T(128)S(1)} %get-tuple-element.140, f32[128]{0:T(128)S(1)} %get-tuple-element.139), channel_id=1, replica_groups=mesh['dp'=4,'vocab'=8] {'vocab'}, use_global_device_ids=true, to_apply=%region_12.13 | all-reduce | flops 256 | bytes 2048 | tf_op jit(solution)/shard_map/psum | solution.py:70
  177.6 0.0 copy-start.4
  177.6 0.0 copy-done.3
  177.6 0.6 multiply_reduce_fusion
  178.2 6.3 %all-reduce.1 = (f32[]{:T(128)}, f32[]{:T(128)}) all-reduce(f32[]{:T(128)} %get-tuple-element.142, f32[]{:T(128)} %get-tuple-element.141), channel_id=1, replica_groups=mesh['dp'=4,'vocab'=8] {'dp'}, use_global_device_ids=true, to_apply=%region_1.2 | all-reduce | flops 2 | bytes 16 | tf_op jit(solution)/shard_map/psum | solution.py:45
  184.4 0.6 convert_divide_fusion
  185.1 8.2 %fusion.10 = f32[128,2048]{1,0:T(8,128)} fusion(bf16[2048,2432]{1,0:T(8,128)(2,1)} %bitcast.47, bf16[128,2432]{0,1:T(8,128)(2,1)S(1)} %copy.10, f32[2432,128]{1,0:T(8,128)S(1)} %get-tuple-element.162, f32[128]{0:T(128)S(1)} %log.7, f32[128]{0:T(128)S(1)} %pmax.7, f32[128]{0:T(128)S(1)} %log.6, f32[128]{0:T(128)S(1)} %get-tuple-element.137, ...), kind=kOutput, calls=%fused_computation.23 | convolution fusion | flops 1277558784 | bytes 12880384 | tf_op jit(solution)/shard_map/dot_general | solution.py:74
  193.3 0.0 copy-done.4
  193.3 0.0 reduce-scatter.2.cloned.1.call-update
  194.7 61.0 %reduce-scatter.2.cloned.1.call-done = f32[128,256]{1,0:T(8,128)} async-done(((f32[128,2048]{1,0:T(8,128)}), f32[128,256]{1,0:T(8,128)}) %reduce-scatter.2.cloned.1.call-update) | async-done | bytes 131088 | tf_op jit(solution)/shard_map/reduce_scatter | solution.py:77
  255.7 1.5 convert_element_type.16
  (12 shorter events, 0.2 us)
Async XLA Ops:
  7.2 107.5 %all-gather.6.cloned.1.call-start = ((), (), s32[]{:S(2)}) async-start(), calls=%async_computation.1 | async-start | bytes 12451840 | tf_op jit(solution)/shard_map/all_gather | solution.py:54
  10.1 30.5 %collective-permute-start = (bf16[256,2432]{1,0:T(8,128)(2,1)}, bf16[256,2432]{1,0:T(8,128)(2,1)S(1)}, u32[]{:S(2)}, u32[]{:S(2)}) collective-permute-start(bf16[256,2432]{1,0:T(8,128)(2,1)} %get-tuple-element.160), channel_id=1, source_target_pairs={{0,1},{1,0},{2,3},{3,2},{4,5},{5,4},{6,7},{7,6},{8,9},{9,8},{10,11... | collective-permute-start | bytes 3735560 | tf_op jit(solution)/shard_map/ppermute | solution.py:11
  42.5 1.1 copy-start
  42.5 213.1 %reduce-scatter.2.cloned.1.call-start = ((), (), s32[]{:S(2)}) async-start(), calls=%async_computation.2 | async-start | bytes 1179648 | tf_op jit(solution)/shard_map/reduce_scatter | solution.py:77
  43.6 39.9 %copy-start.1 = (bf16[128,256]{1,0:T(8,128)(2,1)S(1)}, bf16[128,256]{1,0:T(8,128)(2,1)}, u32[]{:S(2)}) copy-start(bf16[128,256]{1,0:T(8,128)(2,1)} %param.7) | copy-start | bytes 196612
  121.4 35.4 %copy-start.2 = (s32[128]{0:T(128)S(1)}, s32[128]{0:T(128)}, u32[]{:S(2)}) copy-start(s32[128]{0:T(128)} %param.10) | copy-start | bytes 1540
  121.7 55.9 %copy-start.3 = (s32[128]{0:T(128)S(1)}, s32[128]{0:T(128)}, u32[]{:S(2)}) copy-start(s32[128]{0:T(128)} %param.11) | copy-start | bytes 1540
  177.6 15.8 %copy-start.4 = (f32[128]{0:T(128)}, f32[128]{0:T(128)S(1)}, u32[]{:S(2)}) copy-start(f32[128]{0:T(128)S(1)} %get-tuple-element.153) | copy-start | bytes 1540
Sparse Core Ops, SparseCore 0:
  42.6 68.6 all-gather.5
  193.5 62.1 reduce-scatter.1
where the time goes:
time: 266 us; the launch traced here: 265 us
  blocking collectives  131 us (49%)
  waiting for transfers between devices  88.6 us (33%)
  between operations  16.6 us (6%)
  matrix products  14.9 us (6%)
  other arithmetic  6.81 us (3%)
  local copies, waits for them, and re-layouts  4.23 us (2%)
  starting transfers between devices  3.05 us (1%)
    reduce_scatter x1, waiting for transfers between devices, on_device(): lax.psum_scatter(term, 'vocab', scatter_dimension=1, tiled=True)  61 us
    all_gather x2, blocking collectives, combined_all(): gathered = jax.tree.map(lambda a: lax.all_gather(a, axis), part)  34.7 us
    all_gather x1, blocking collectives, on_device(): gathered = lax.all_gather(student_hidden, 'vocab', axis=1, tiled=True)  31.2 us
    ppermute x1, waiting for transfers between devices, swapped(): lax.ppermute(shard, axis, [(i, i ^ 1 << stride) for i in range(lax.axis_s...  27.6 us
    pmax x1, blocking collectives, on_device(): teacher_max = lax.pmax(jnp.max(teacher_full, axis=1), 'vocab')  21.9 us
    psum x1, blocking collectives, on_device(): token_kl, sampled = lax.psum((kl_part, sampled_part), 'vocab')  19.7 us
    psum x1, blocking collectives, on_device(): lax.psum(jnp.sum(jnp.exp(teacher_full - teacher_max[:, None]), axis=1), '...  17.1 us
    dot_general x1, matrix products, on_device(): lax.dot_general(dlogits, weight, (((1,), (1,)), ((), ())), preferred_elem...  8.22 us
  transfers between devices with their start and end apart: 3, of which 2 were waited for; matrix products, arithmetic and copies ran while one was open for 0% of the time, Pallas kernels for 0%

commit v1 on v0

--- a/solution.py
+++ b/solution.py
@@ -43,7 +43,9 @@
     pair_side = vocab_index % 2
     mask_float = loss_mask.astype(jnp.float32)
     mask_total = lax.psum(jnp.sum(mask_float), "dp")
-    gathered = lax.all_gather(student_hidden, "vocab", axis=1, tiled=True)
+    gathered = jnp.concatenate(
+        lax.all_to_all(jnp.stack([student_hidden] * lax.axis_size("vocab")), "vocab", 0, 0), axis=1
+    )
     piece = student_blocks[0]
     own_block = lax.dynamic_slice_in_dim(piece, pair_side * VT, VT, 1)
     far_block = lax.dynamic_slice_in_dim(piece, (1 - pair_side) * VT, VT, 1)

time: 266 us -> 263 us (0.989)
  blocking collectives: 131 us -> 104 us
  waiting for transfers between devices: 88.6 us -> 106 us
  starting transfers between devices: 3.05 us -> 9.1 us
    all_gather x1 -> x0, blocking collectives: 31.2 us -> none  [on_device(): gathered = lax.all_gather(student_hidden, 'vocab', axis=1, tiled=True)]
    all_gather x1, waiting for transfers between devices: 0.01 us -> 19.1 us  [on_device(): weight = lax.all_gather(stacked, 'dp', axis=1, tiled=True).reshape(D, VT)]
    all_to_all x0 -> x1, starting transfers between devices: none -> 6.06 us  [on_device(): lax.all_to_all(jnp.stack([student_hidden] * lax.axis_size('vocab')), 'voc...]
  transfers between devices with their start and end apart: 3 -> 4, of which waited for: 2 -> 3; matrix products, arithmetic and copies ran while one was open for 0% -> 1% of each run, Pallas kernels for 0% -> 0%
where the time goes in v1:
time: 263 us
  waiting for transfers between devices  106 us (40%)
  blocking collectives  104 us (40%)
  between operations  16.6 us (6%)
  matrix products  14.8 us (6%)
  starting transfers between devices  9.1 us (3%)
  other arithmetic  6.81 us (3%)
  local copies, waits for them, and re-layouts  5.05 us (2%)
    reduce_scatter x1, waiting for transfers between devices, on_device(): lax.psum_scatter(term, 'vocab', scatter_dimension=1, tiled=True)  59.5 us
    all_gather x2, blocking collectives, combined_all(): gathered = jax.tree.map(lambda a: lax.all_gather(a, axis), part)  36.9 us
    ppermute x1, waiting for transfers between devices, swapped(): lax.ppermute(shard, axis, [(i, i ^ 1 << stride) for i in range(lax.axis_s...  27.6 us
    pmax x1, blocking collectives, on_device(): teacher_max = lax.pmax(jnp.max(teacher_full, axis=1), 'vocab')  22.1 us
    psum x1, blocking collectives, on_device(): token_kl, sampled = lax.psum((kl_part, sampled_part), 'vocab')  19.7 us
    all_gather x1, waiting for transfers between devices, on_device(): weight = lax.all_gather(stacked, 'dp', axis=1, tiled=True).reshape(D, VT)  19.1 us
    psum x1, blocking collectives, on_device(): lax.psum(jnp.sum(jnp.exp(teacher_full - teacher_max[:, None]), axis=1), '...  18.9 us
    dot_general x1, matrix products, on_device(): lax.dot_general(dlogits, weight, (((1,), (1,)), ((), ())), preferred_elem...  8.2 us
  transfers between devices with their start and end apart: 4, of which 3 were waited for; matrix products, arithmetic and copies ran while one was open for 1% of the time, Pallas kernels for 0%

profile of v1, /device:TPU:0, one launch (start us, length us, event | category | flops | bytes accessed | tf_op | source)
XLA Modules:
  0.0 262.8 jit_solution(11672858103054976847)
XLA Ops:
  7.2 0.0 all-gather.6.cloned.1.call-start
  7.2 2.9 %constant_dynamic-slice_fusion.1 = (bf16[1,256,2432]{2,1,0:T(8,128)(2,1)S(1)}, bf16[256,2432]{1,0:T(8,128)(2,1)}) fusion(bf16[1,256,4864]{2,1,0:T(8,128)(2,1)} %param.8, s32[]{:T(128)S(6)} %select_n.41, s32[]{:T(128)S(6)} %select_n.42), kind=kLoop, calls=%fused_computation.33 | loop fusion | bytes 4980744 | tf_op jit(solution)/shard_map/dynamic_slice | solution.py:50
  10.1 3.0 %collective-permute-start = (bf16[256,2432]{1,0:T(8,128)(2,1)}, bf16[256,2432]{1,0:T(8,128)(2,1)S(1)}, u32[]{:S(2)}, u32[]{:S(2)}) collective-permute-start(bf16[256,2432]{1,0:T(8,128)(2,1)} %get-tuple-element.160), channel_id=1, source_target_pairs={{0,1},{1,0},{2,3},{3,2},{4,5},{5,4},{6,7},{7,6},{8,9},{9,8},{10,11... | collective-permute-start | bytes 3735560 | tf_op jit(solution)/shard_map/ppermute | solution.py:11
  13.1 27.6 %collective-permute-done = bf16[256,2432]{1,0:T(8,128)(2,1)S(1)} collective-permute-done((bf16[256,2432]{1,0:T(8,128)(2,1)}, bf16[256,2432]{1,0:T(8,128)(2,1)S(1)}, u32[]{:S(2)}, u32[]{:S(2)}) %collective-permute-start) | collective-permute-done | bytes 1245216 | tf_op jit(solution)/shard_map/ppermute | solution.py:11
  40.7 1.8 maximum_select_fusion
  42.5 0.0 copy-start.1
  42.5 0.0 all-gather.6.cloned.1.call-update
  42.5 0.8 copy-done.1
  43.3 0.0 copy-start
  43.3 0.1 copy.12
  43.5 0.9 stack.11
  44.3 6.1 %all-to-all-start = ((bf16[8,128,256]{1,2,0:T(8,128)(2,1)}), bf16[8,128,256]{1,2,0:T(8,128)(2,1)S(1)}, u32[]{:S(2)}, u32[]{:S(2)}) async-start(bf16[8,128,256]{1,2,0:T(8,128)(2,1)} %stack.11), calls=%async_computation | async-start | bytes 1048576 | tf_op jit(solution)/shard_map/all_to_all | solution.py:47
  50.4 0.0 reduce-scatter.2.cloned.1.call-start
  50.4 0.0 copy-done
  50.5 0.3 copy.13
  50.8 0.2 reduce_max.24
  51.0 22.1 %pmax.7 = f32[128]{0:T(128)S(1)} all-reduce(bf16[128]{0:T(256)(128)(2,1)S(1)} %reduce_max.24), channel_id=1, replica_groups=mesh['dp'=4,'vocab'=8] {'vocab'}, use_global_device_ids=true, to_apply=%region_7.8 | all-reduce | flops 128 | bytes 768 | tf_op jit(solution)/shard_map/pmax | solution.py:61
  73.1 0.3 exponential_reduce_fusion
  73.4 18.9 %psum.36 = f32[128]{0:T(128)S(1)} all-reduce(f32[128]{0:T(128)S(1)} %exponential_reduce_fusion), channel_id=1, replica_groups=mesh['dp'=4,'vocab'=8] {'vocab'}, use_global_device_ids=true, to_apply=%region_9.10 | all-reduce | flops 128 | bytes 1024 | tf_op jit(solution)/shard_map/psum | solution.py:62
  92.3 0.0 all-to-all-done
  92.3 19.1 %all-gather.6.cloned.1.call-done = bf16[2,1024,2432]{2,1,0:T(8,128)(2,1)} async-done(((bf16[2,256,2432]{2,1,0:T(8,128)(2,1)}), bf16[2,1024,2432]{2,1,0:T(8,128)(2,1)}) %all-gather.6.cloned.1.call-update) | async-done | bytes 9961488 | tf_op jit(solution)/shard_map/all_gather | solution.py:56
  111.4 6.6 %fusion.17 = (f32[128]{0:T(128)S(1)}, f32[2432,128]{1,0:T(8,128)S(1)}) fusion(bf16[2048,2432]{1,0:T(8,128)(2,1)} %bitcast.49, bf16[128,2048]{0,1:T(8,128)(2,1)S(1)} %bitcast.52), kind=kOutput, calls=%fused_computation.36 | convolution fusion | flops 1275379584 | bytes 11731456 | tf_op jit(solution)/shard_map/dot_general | solution.py:57
  118.0 0.0 copy-start.2
  118.0 0.3 exponential_reduce_fusion.1
  118.4 0.0 copy-start.3
  118.4 20.6 %all-gather.3 = f32[8,1,128]{2,1,0:T(1,128)S(1)} all-gather(f32[1,1,128]{2,1,0:T(1,128)S(1)} %bitcast.56), channel_id=3, replica_groups=mesh['dp'=4,'vocab'=8] {'vocab'}, dimensions={0}, use_global_device_ids=true | all-gather | bytes 4608 | tf_op jit(solution)/shard_map/all_gather | solution.py:15
  139.0 16.3 %all-gather.2 = f32[8,1,128]{2,1,0:T(1,128)S(1)} all-gather(f32[1,1,128]{2,1,0:T(1,128)S(1)} %bitcast.55), channel_id=2, replica_groups=mesh['dp'=4,'vocab'=8] {'vocab'}, dimensions={0}, use_global_device_ids=true | all-gather | bytes 4608 | tf_op jit(solution)/shard_map/all_gather | solution.py:15
  155.3 0.3 while.17
  155.6 0.0 copy-done.2
  155.6 1.1 fusion.7
  156.7 19.7 %all-reduce = (f32[128]{0:T(128)S(1)}, f32[128]{0:T(128)}) all-reduce(f32[128]{0:T(128)S(1)} %get-tuple-element.140, f32[128]{0:T(128)S(1)} %get-tuple-element.139), channel_id=1, replica_groups=mesh['dp'=4,'vocab'=8] {'vocab'}, use_global_device_ids=true, to_apply=%region_12.13 | all-reduce | flops 256 | bytes 2048 | tf_op jit(solution)/shard_map/psum | solution.py:72
  176.4 0.0 copy-start.4
  176.4 0.0 copy-done.3
  176.4 0.6 multiply_reduce_fusion
  177.0 6.5 %all-reduce.1 = (f32[]{:T(128)}, f32[]{:T(128)}) all-reduce(f32[]{:T(128)} %get-tuple-element.142, f32[]{:T(128)} %get-tuple-element.141), channel_id=1, replica_groups=mesh['dp'=4,'vocab'=8] {'dp'}, use_global_device_ids=true, to_apply=%region_1.2 | all-reduce | flops 2 | bytes 16 | tf_op jit(solution)/shard_map/psum | solution.py:45
  183.6 0.6 convert_divide_fusion
  184.2 8.2 %fusion.10 = f32[128,2048]{1,0:T(8,128)} fusion(bf16[2048,2432]{1,0:T(8,128)(2,1)} %bitcast.50, bf16[128,2432]{0,1:T(8,128)(2,1)S(1)} %copy.13, f32[2432,128]{1,0:T(8,128)S(1)} %get-tuple-element.162, f32[128]{0:T(128)S(1)} %log.7, f32[128]{0:T(128)S(1)} %pmax.7, f32[128]{0:T(128)S(1)} %log.6, f32[128]{0:T(128)S(1)} %get-tuple-element.137, ...), kind=kOutput, calls=%fused_computation.23 | convolution fusion | flops 1277558784 | bytes 12880384 | tf_op jit(solution)/shard_map/dot_general | solution.py:76
  192.4 0.0 copy-done.4
  192.4 0.0 reduce-scatter.2.cloned.1.call-update
  193.8 59.5 %reduce-scatter.2.cloned.1.call-done = f32[128,256]{1,0:T(8,128)} async-done(((f32[128,2048]{1,0:T(8,128)}), f32[128,256]{1,0:T(8,128)}) %reduce-scatter.2.cloned.1.call-update) | async-done | bytes 131088 | tf_op jit(solution)/shard_map/reduce_scatter | solution.py:79
  253.3 1.5 convert_element_type.16
  (12 shorter events, 0.2 us)
Async XLA Ops:
  7.2 104.2 %all-gather.6.cloned.1.call-start = ((), (), s32[]{:S(2)}) async-start(), calls=%async_computation.2 | async-start | bytes 12451840 | tf_op jit(solution)/shard_map/all_gather | solution.py:56
  10.1 30.5 %collective-permute-start = (bf16[256,2432]{1,0:T(8,128)(2,1)}, bf16[256,2432]{1,0:T(8,128)(2,1)S(1)}, u32[]{:S(2)}, u32[]{:S(2)}) collective-permute-start(bf16[256,2432]{1,0:T(8,128)(2,1)} %get-tuple-element.160), channel_id=1, source_target_pairs={{0,1},{1,0},{2,3},{3,2},{4,5},{5,4},{6,7},{7,6},{8,9},{9,8},{10,11... | collective-permute-start | bytes 3735560 | tf_op jit(solution)/shard_map/ppermute | solution.py:11
  42.5 0.8 copy-start.1
  43.3 7.1 %copy-start = (bf16[128,2432]{1,0:T(8,128)(2,1)S(1)}, bf16[128,2432]{1,0:T(8,128)(2,1)}, u32[]{:S(2)}) copy-start(bf16[128,2432]{1,0:T(8,128)(2,1)} %param.9) | copy-start | bytes 1867780
  44.3 48.0 %all-to-all-start = ((bf16[8,128,256]{1,2,0:T(8,128)(2,1)}), bf16[8,128,256]{1,2,0:T(8,128)(2,1)S(1)}, u32[]{:S(2)}, u32[]{:S(2)}) async-start(bf16[8,128,256]{1,2,0:T(8,128)(2,1)} %stack.11), calls=%async_computation | async-start | bytes 1048576 | tf_op jit(solution)/shard_map/all_to_all | solution.py:47
  50.4 202.9 %reduce-scatter.2.cloned.1.call-start = ((), (), s32[]{:S(2)}) async-start(), calls=%async_computation.3 | async-start | bytes 1179648 | tf_op jit(solution)/shard_map/reduce_scatter | solution.py:79
  118.0 37.6 %copy-start.2 = (s32[128]{0:T(128)S(1)}, s32[128]{0:T(128)}, u32[]{:S(2)}) copy-start(s32[128]{0:T(128)} %param.10) | copy-start | bytes 1540
  118.4 58.0 %copy-start.3 = (s32[128]{0:T(128)S(1)}, s32[128]{0:T(128)}, u32[]{:S(2)}) copy-start(s32[128]{0:T(128)} %param.11) | copy-start | bytes 1540
  176.4 16.0 %copy-start.4 = (f32[128]{0:T(128)}, f32[128]{0:T(128)S(1)}, u32[]{:S(2)}) copy-start(f32[128]{0:T(128)S(1)} %get-tuple-element.153) | copy-start | bytes 1540
Sparse Core Ops, SparseCore 0:
  42.6 68.7 all-gather.5
  192.6 60.6 reduce-scatter.1
